TPU v7x, 32 devices: a whole 2x2x4 slice. The times are simulated.
32 devices in a mesh: tp: 8 (over z, y), dp: 4 (over x, core).
Axes of the slice: x: 2, y: 2, z: 4, core: 2. Of those that a mesh axis runs over, the one named last changes fastest.
Arguments:
- x: bfloat16 [8192, 2048], P(('dp', 'tp'))
- w_gate: bfloat16 [2048, 8192], P('dp', 'tp')
- w_up: bfloat16 [2048, 8192], P('dp', 'tp')
- w_down: bfloat16 [8192, 2048], P('tp', 'dp')
- dy: bfloat16 [8192, 2048], P(('dp', 'tp'))
Outputs:
- output 1: bfloat16 [8192, 2048], P(('dp', 'tp'))
- output 2: bfloat16 [8192, 2048], P(('dp', 'tp'))
- output 3: float32 [2048, 8192], P('dp', 'tp')
- output 4: float32 [2048, 8192], P('dp', 'tp')
- output 5: float32 [8192, 2048], P('tp', 'dp')
All inputs are finite; a program needn't handle non-finite values.
Results may differ from a plain program's by a relative error of at most 0.00111.
Values are sent between devices in bfloat16 or wider.
A program may use at most 1 GiB of HBM per device.

v0:
```python
import jax
import jax.numpy as jnp
from jax import lax
from jax.experimental import pallas as pl
from jax.experimental.pallas import tpu as pltpu
from jax.sharding import PartitionSpec as P

MESH = pl.DeviceIdType.MESH
f32 = jnp.float32
bf = jnp.bfloat16
VMEM_LIMIT = 67043328
sc = jax.named_scope
LAG = 4


def mm(a, b):
    return lax.dot_general(a, b, (((1,), (0,)), ((), ())), preferred_element_type=f32)


def mmt(a, b):
    return lax.dot_general(a, b, (((1,), (1,)), ((), ())), preferred_element_type=f32)


def natural(dp, r, kd):
    x, c, rc, rx = dp // 2, dp % 2, r // 2, r % 2
    n = 2 * (x + rx - 2 * x * rx) + c + rc - 2 * c * rc
    return pl.ds(pl.multiple_of(n * kd, kd), kd)


def kernel(
    x_in, dy_in, wg_in, wu_in, wd_in,
    xa, dya, dwv, zl, n00, r2, far_r, near, xr1, yr1, stash,
    wg, wu, wd, act, zs, xt, ht, eye, cst,
    gs, gr, lsem, zsend, zrecv, zload, fsend, frecv, nstore, cload, xs1, xq1, ys1, yq1, s2, q2, cin, ssem,
):
    tp = lax.axis_index("tp")
    dp = lax.axis_index("dp")
    z, y = tp // 2, tp % 2
    x, c = dp // 2, dp % 2
    is_end = (z == 0) | (z == 3)
    is_mid = (z == 1) | (z == 2)
    dev_x = {"tp": tp, "dp": 2 * (1 - x) + c}
    dev_y = {"tp": 2 * z + 1 - y, "dp": dp}
    dev_c = {"tp": tp, "dp": 2 * x + 1 - c}
    dev_a = {"tp": 2 * (z + 1 - 2 * (z % 2)) + y, "dp": dp}
    dev_b = {"tp": 2 * (3 - z) + y, "dp": dp}

    fst, nst = dwv.at[pl.ds(0, 3)], dwv.at[pl.ds(3, 2)]
    nr, d = x_in.shape
    kd, kf = wg_in.shape
    f = 2 * kf
    hd = kd // 2
    hf = kf // 2

    def end(fn):
        pl.when(is_end)(fn)

    def mid(fn):
        pl.when(is_mid)(fn)

    def ncol(r):
        return natural(dp, r, kd)

    def remote(src, dst, ss, rs, dev):
        return pltpu.make_async_remote_copy(
            src_ref=src, dst_ref=dst, send_sem=ss, recv_sem=rs, device_id=dev, device_id_type=MESH
        )

    own = (wg_in, wu_in, wd_in)

    def blk(k, rx, rc, ry, lo=0, n=None):
        d0 = (2 * rc + rx) * kd + lo
        n = kd if n is None else n
        if k < 2:
            return (wg, wu)[k].at[pl.ds(d0, n), pl.ds(ry * kf, kf)]
        return wd.at[pl.ds(ry * kf, kf), pl.ds(d0, n)]

    local = [(own[k], blk(k, 0, 0, 0)) for k in range(3)]
    for src, ref in ((x_in, xa), (dy_in, dya)):
        for r in range(4):
            local.append((src.at[:, ncol(r)], ref.at[pl.ds(0, nr), pl.ds(r * kd, kd)]))
    local = [pltpu.make_async_copy(s, t, lsem.at[i]) for i, (s, t) in enumerate(local)]
    for cp in local:
        cp.start()

    bar = pltpu.get_barrier_semaphore()
    for dev in (dev_x, dev_y, dev_c, dev_a, dev_b):
        pl.semaphore_signal(bar, inc=1, device_id=dev, device_id_type=MESH)

    with sc("barrier"):
        pl.semaphore_wait(bar, 5)

    ft = min(256, f)

    def rows(s):
        return pl.ds(s * nr, nr)

    def transpose_x(rx, lo, hi):
        @pl.loop(lo, hi)
        def _(s):
            row = pl.ds(pl.multiple_of(s * nr, nr), nr)
            for rc in range(2):
                for h in range(2):
                    v = mmt(eye[...], xa[row, pl.ds((2 * rc + rx) * kd + h * hd, hd)])
                    xt[rc, pl.ds(h * hd, hd), row] = v.astype(bf)

    def wcopy(i, src, dst, dev):
        return remote(src, dst, gs.at[i], gr.at[i], dev)

    def half(rx, rc, ry, h):
        return blk(2, rx, rc, ry, h * hd, hd)

    ua = 3 * kd // 4
    mine = [blk(k, 0, 0, 0) for k in range(3)]
    xo = [wcopy(k, mine[k], blk(k, 1, 0, 0), dev_x) for k in range(2)]
    yo = [wcopy(2 + k, mine[k], blk(k, 0, 0, 1), dev_y) for k in range(2)]
    co = [wcopy(4 + k, mine[k], blk(k, 0, 1, 0), dev_c) for k in range(3)]
    xd = [wcopy(7 + h, half(0, 0, 0, h), half(1, 0, 0, h), dev_x) for h in range(2)]
    yd = [wcopy(9 + h, half(0, 0, 0, h), half(0, 0, 1, h), dev_y) for h in range(2)]
    rg = wcopy(11, blk(0, 0, 0, 1), blk(0, 1, 0, 1), dev_x)
    ay, ax = ((0, 5 * kd // 8), (5 * kd // 8, ua)), ((ua, 7 * kd // 8), (7 * kd // 8, kd))
    rua = [wcopy(i, blk(1, 1, 0, 0, lo, hi - lo), blk(1, 1, 0, 1, lo, hi - lo), dev_y) for i, (lo, hi) in zip((12, 29), ay)]
    rub = [wcopy(i, blk(1, 0, 0, 1, lo, hi - lo), blk(1, 1, 0, 1, lo, hi - lo), dev_x) for i, (lo, hi) in zip((13, 31), ax)]
    rd = [wcopy(14 + h, half(1, 0, 0, h), half(1, 0, 1, h), dev_y) for h in range(2)]
    cx = [wcopy(16 + k, blk(k, 1, 0, 0), blk(k, 1, 1, 0), dev_c) for k in range(2)]
    cy = [wcopy(18 + k, blk(k, 0, 0, 1), blk(k, 0, 1, 1), dev_c) for k in range(2)]
    cxd = [wcopy(20 + h, half(1, 0, 0, h), half(1, 1, 0, h), dev_c) for h in range(2)]
    cyd = [wcopy(22 + h, half(0, 0, 1, h), half(0, 1, 1, h), dev_c) for h in range(2)]
    crg = wcopy(24, blk(0, 1, 0, 1), blk(0, 1, 1, 1), dev_c)
    crua = [wcopy(i, blk(1, 1, 0, 1, lo, hi - lo), blk(1, 1, 1, 1, lo, hi - lo), dev_c) for i, (lo, hi) in zip((25, 30), ay)]
    crub = [wcopy(i, blk(1, 1, 0, 1, lo, hi - lo), blk(1, 1, 1, 1, lo, hi - lo), dev_c) for i, (lo, hi) in zip((26, 32), ax)]
    crd = [wcopy(27 + h, half(1, 0, 1, h), half(1, 1, 1, h), dev_c) for h in range(2)]
    wcopies = (*xo, *yo, *co, *xd, *yd, rg, *rua, *rub, *rd, *cx, *cy, *cxd, *cyd, crg, *crua, *crub, *crd)
    nw = 33

    def slot(j, s):
        return (xa, dya)[j].at[pl.ds(s * nr, nr)]

    def acopy(src, dst, j):
        return remote(
            slot(j, src), slot(j, dst), gs.at[nw + 2 * dst + j], gr.at[nw + 2 * dst + j], dev_a
        )

    def bcopy(src, dst, j):
        return remote(
            slot(j, src), slot(j, dst), gs.at[nw + 8 + 2 * dst + j], gr.at[nw + 2 * dst + j], dev_b
        )

    def got(s, j):
        acopy(s, s, j).wait_recv()

    def stash_copy(s, p, n):
        return pltpu.make_async_copy((fst, nst)[n].at[p, pl.ds(0, nr)], stash.at[s, p, n], ssem.at[2 * p + n])

    def factor(s, n):
        return nst if n else cst if s == 3 else fst

    def stash_load(s, p, n):
        return pltpu.make_async_copy(stash.at[s, p, n], factor(s, n).at[p, pl.ds(0, nr)], ssem.at[2 * p + n])

    pending = [None, None]

    def flush(p):
        if pending[p] is not None:
            for n in range(2):
                stash_copy(pending[p], p, n).wait()
        pending[p] = None

    def ab_tiles(s, p, step):
        def tile(i):
            col = pl.ds(pl.multiple_of(p * kf + i * ft, ft), ft)
            at = (p, pl.ds(0, nr), pl.ds(pl.multiple_of(i * ft, ft), ft))

            def some_b(rx):
                b0, b1 = pl.ds(rx * kd, kd), pl.ds((2 + rx) * kd, kd)
                return mm(xa[rows(s), b0], wu[b0, col]) + mm(xa[rows(s), b1], wu[b1, col])

            if step == 1:
                fst[at] = mm(xa[rows(s), :], wg[:, col])
                nst[at] = some_b(0)
                return
            if step == 2:
                a = fst[at]
                b = nst[at] + some_b(1)
            else:
                a = mm(xa[rows(s), :], wg[:, col])
                b = mm(xa[rows(s), :], wu[:, col])
            sig = jax.nn.sigmoid(a)
            sa = a * sig
            act[2, rows(s), col] = (sa * b).astype(bf)
            fst[at] = sa
            nst[at] = b * sig * (1.0 + a * (1.0 - sig))

        m = 2 if step == 2 and kf // ft > 1 else 1

        @pl.loop(0, kf // ft // m)
        def _(i):
            for q in range(m):
                tile(i * m + q)

    def part_ab(s, p, step=0):
        with sc(f"ab{s}_{p}"):
            flush(p)
            ab_tiles(s, p, step)
            if step != 1:
                for n in range(2):
                    stash_copy(s, p, n).start()
                pending[p] = s

    gt = min(512, kf)

    def part_g(s, p):
        @pl.loop(0, kf // gt)
        def _(i):
            col = pl.ds(pl.multiple_of(p * kf + i * gt, gt), gt)
            kcol = pl.ds(pl.multiple_of(i * gt, gt), gt)
            g = mmt(dya[rows(s), :], wd[col, :])
            act[0, rows(s), col] = (g * factor(s, 1)[p, pl.ds(0, nr), kcol]).astype(bf)
            act[1, rows(s), col] = (g * factor(s, 0)[p, pl.ds(0, nr), kcol]).astype(bf)

    def gload(s):
        for p in range(2):
            for n in range(2):
                stash_load(s, p, n).start()

    def half_g(s, p, then):
        with sc(f"g{s}"):
            for n in range(2):
                stash_load(s, p, n).wait()
            part_g(s, p)
            if then is not None:
                for n in range(2):
                    stash_load(then, p, n).start()

    def front_g(s, then):
        @pl.loop(0, 2)
        def _(p):
            half_g(s, p, then)

    def keep_h(lo, hi):
        hb = min(4, f // hd)
        nh = f // (hb * hd)
        with sc("ht"):
            @pl.loop(lo * nh, hi * nh)
            def _(i):
                row = pl.ds(pl.multiple_of(i // nh * nr, nr), nr)
                for q in range(hb):
                    col = pl.ds(pl.multiple_of((i % nh * hb + q) * hd, hd), hd)
                    ht[col, row] = mmt(eye[...], act[2, row, col]).astype(bf)

    def back(ref, at, kind, s, r):
        *lead, c0 = at

        @pl.loop(0, 2)
        def _(h):
            n = pl.ds(pl.multiple_of(r * kd + h * hd, hd), hd)
            if kind == 0:
                v = mm(act[2, rows(s), :], wd[:, n])
            else:
                v = mmt(act[0, rows(s), :], wg[n, :]) + mmt(act[1, rows(s), :], wu[n, :])
            ref[(*lead, pl.ds(0, nr), pl.ds(pl.multiple_of(c0 + h * hd, hd), hd))] = v

    def zcopy(q, kind, r, half, dev):
        i = 4 * kind + r
        return remote(zs.at[4 * half + r], zl.at[q, i], zsend.at[4 * half + r], zrecv.at[q, i], dev)

    def zload_(q, kind, r, slot):
        return pltpu.make_async_copy(zl.at[q, 4 * kind + r], cst.at[slot, pl.ds(0, nr), pl.ds(0, kd)], zload.at[slot])

    def chunk(kind, s, r, half, q_add, first):
        i = 4 * half + r
        if q_add is not None:
            with sc("zrecv"):
                zcopy(q_add, kind, r, half, dev_a).wait_recv()
            zload_(q_add, kind, r, r % 2).start()
        if not first:
            with sc("zsend"):
                zcopy(0, kind, r, half, dev_a).wait_send()
        back(zs, (i, 0), kind, s, r)
        if q_add is not None:
            zload_(q_add, kind, r, r % 2).wait()
            zs[i] = zs[i] + cst[r % 2, pl.ds(0, nr), pl.ds(0, kd)]

    def jobs(*specs):
        with sc("job" + "_".join(f"{kind}{s}" for kind, s, *_ in specs)):
            @pl.loop(0, 4)
            def _(r):
                for kind, s, h, q_add, q_dst, dev, first in specs:
                    chunk(kind, s, r, h, q_add, first)
                    zcopy(q_dst, kind, r, h, dev).start()

    def last_part():
        back(cst, (0, kd), 1, 0, 3)
        at = (0, pl.ds(0, nr), pl.ds(kd, kd))
        cst[at] = cst[at] + dya[rows(0), pl.ds(3 * kd, kd)].astype(f32)
        cp = pltpu.make_async_copy(cst.at[at], zl.at[1, 7], zload.at[0])
        cp.start()
        cp.wait()

    def finish(kind, adds, lo=0, hi=4):
        res = (xa, dya)[kind]
        with sc(f"fin{kind}"):
            @pl.loop(lo, hi)
            def _(r):
                col = pl.ds(pl.multiple_of(r * kd, kd), kd)
                part = (pl.ds(0, nr), pl.ds(0, kd))
                temp = (0, pl.ds(0, nr), pl.ds(kd, kd))
                back(cst, (0, kd), kind, 0, r)
                for n, q in enumerate(adds):
                    with sc("finrecv"):
                        zcopy(q, kind, r, 0, dev_a).wait_recv()
                    zload_(q, kind, r, n).start()
                for n, q in enumerate(adds):
                    zload_(q, kind, r, n).wait()
                v = cst[temp] + res[rows(0), col].astype(f32)
                for n in range(len(adds)):
                    v = v + cst[n, *part]
                res[rows(1), col] = v.astype(bf)

    def unit(rc, rx, j, put):
        ryi, k, half = j // 6, ((j // 2) % 3 + 2) % 3, j % 2
        f0 = (1 - ryi) * kf

        @pl.when(k < 2)
        def _():
            a = xt[rc, pl.ds(pl.multiple_of(half * hd, hd), hd), :]
            for q in range(4):
                b = act[k, :, pl.ds(pl.multiple_of(f0 + q * hd, hd), hd)]
                put(pl.ds(q * hd, hd), mm(a, b))

        @pl.when(k == 2)
        def _():
            for q in range(4):
                b = dya[:, pl.ds((2 * rc + rx) * kd + q % 2 * hd, hd)]
                a = ht[pl.ds(pl.multiple_of(f0 + half * hf + q // 2 * hd, hd), hd), :]
                put(pl.ds(q * hd, hd), mm(a, b))

    def fcopy(u):
        return remote(fst.at[u % 3], far_r.at[u], fsend.at[u % 3], frecv.at[u], dev_c)

    def ncopy(u):
        return pltpu.make_async_copy(nst.at[(u + 1) % 2], near.at[u], nstore.at[(u + 1) % 2])

    def ccopy(u):
        return pltpu.make_async_copy(far_r.at[u], cst.at[(u + 1) % 2], cload.at[(u + 1) % 2])

    def xcopy1(i, u):
        return remote(near.at[u], xr1.at[i], xs1.at[i], xq1.at[i], dev_x)

    def ycopy1(i, u):
        return remote(near.at[u], yr1.at[i], ys1.at[i], yq1.at[i], dev_y)

    def nsend(rx, j):
        ryi, k, half = j // 6, (j // 2) % 3, j % 2
        u = 12 * (1 - rx) + j
        if rx:
            @pl.when(half == 0)
            def _():
                xcopy1(ryi * 3 + k, u).start()

        @pl.when((half == 1) & (ryi == 0))
        def _():
            ycopy1(3 * (1 - rx) + k, u).start()

    def far_unit(rx, j):
        u = 12 * (1 - rx) + j

        @pl.when(u > 2)
        def _():
            with sc("fsend"):
                fcopy(u).wait_send()

        def put(col, v):
            fst[u % 3, :, col] = v

        unit(1, rx, j, put)
        fcopy(u).start()

    def far_start(lo, hi):
        t = pl.ds(lo * nr, (hi - lo) * nr)
        with sc("farstart"):
            @pl.loop(0, 2)
            def _(j):
                for q in range(4):
                    a = ht[pl.ds(pl.multiple_of(kf + j * hf + q // 2 * hd, hd), hd), t]
                    v = mm(a, dya[t, pl.ds(3 * kd + q % 2 * hd, hd)])
                    at = (j, slice(None), pl.ds(q * hd, hd))
                    fst[at] = fst[at] + v if lo else v

                if lo:
                    fcopy(j).start()

    def near_load(rx, j):
        u = 12 * (1 - rx) + j
        with sc("frecv"):
            fcopy(u).wait_recv()
        ccopy(u).start()

    def near_unit(rx, j):
        u = 12 * (1 - rx) + j
        with sc("cwait"):
            ccopy(u).wait()

        def put(col, v):
            i = (u + 1) % 2
            nst[i, :, col] = v + cst[i, :, col]

        unit(0, rx, j, put)

    def near_done(rx, j):
        with sc("nwait"):
            ncopy(12 * (1 - rx) + j).wait()
        nsend(rx, j)

    def dw(rx, f0, n0):
        base = 12 * (1 - rx)

        with sc(f"dw{rx}"):
            @pl.loop(f0, 12 + LAG)
            def _(j):
                n = j - LAG

                @pl.when(j < 12)
                def _():
                    far_unit(rx, j)

                @pl.when((n + 1 >= n0) & (n < 11))
                def _():
                    near_load(rx, n + 1)

                @pl.when(n >= n0)
                def _():
                    near_unit(rx, n)

                    @pl.when(n > n0)
                    def _():
                        near_done(rx, n - 1)

                    ncopy(base + n).start()

            near_done(rx, 11)

    def add_pair(units, waits, arrived, dsts, after=(None, None)):
        cn = [pltpu.make_async_copy(near.at[u], fst.at[h], cin.at[h]) for h, u in enumerate(units)]
        cr = [pltpu.make_async_copy(v, cst.at[h], cload.at[h]) for h, v in enumerate(arrived)]
        cd = [pltpu.make_async_copy(nst.at[h], t, nstore.at[h]) for h, t in enumerate(dsts)]
        st = min(64, hd)
        for h in range(2):
            cn[h].start()
        for h in range(2):
            waits[h].wait_recv()
            cr[h].start()
        for h in range(2):
            cn[h].wait()
            cr[h].wait()

            @pl.loop(0, hd // st)
            def _(i):
                row = pl.ds(pl.multiple_of(i * st, st), st)
                nst[h, row, :] = fst[h, row, :] + cst[h, row, :]

            cd[h].start()
        for h in range(2):
            cd[h].wait()
            if after[h] is not None:
                after[h].start()

    def uid(rx, ry, k, half):
        return 12 * (1 - rx) + 6 * (1 - ry) + 2 * k + half

    def ycopy2(k):
        return remote(near.at[uid(0, 1, k, 0)], r2.at[2 * k], s2.at[2 * k], q2.at[2 * k], dev_y)

    def xcopy2(k):
        return remote(near.at[uid(1, 0, k, 1)], r2.at[2 * k + 1], s2.at[2 * k + 1], q2.at[2 * k + 1], dev_x)

    def second(k):
        ua, ub = uid(0, 1, k, 0), uid(1, 0, k, 1)
        with sc(f"second{k}"):
            add_pair(
                (ua, ub), (xcopy1(k, 0), ycopy1(k, 0)), (xr1.at[k], yr1.at[k]), (near.at[ua], near.at[ub]),
                (ycopy2(k), xcopy2(k)),
            )

    def third(k):
        ua, ub = uid(0, 0, k, 0), uid(0, 0, k, 1)
        with sc(f"third{k}"):
            add_pair(
                (ua, ub), (xcopy1(3 + k, 0), ycopy1(3 + k, 0)), (xr1.at[3 + k], yr1.at[3 + k]),
                (n00.at[2 * k], n00.at[2 * k + 1]),
            )

    def fourth(k):
        cn = [pltpu.make_async_copy(n00.at[2 * k + h], dwv.at[2 * k + h], cin.at[h]) for h in range(2)]
        cr = [pltpu.make_async_copy(r2.at[2 * k + h], cst.at[h], cload.at[h]) for h in range(2)]
        st = min(64, hd)
        with sc(f"fourth{k}"):
            for h in range(2):
                cn[h].start()
            for h in range(2):
                (ycopy2, xcopy2)[h](k).wait_recv()
                cr[h].start()
            for h in range(2):
                cn[h].wait()
                cr[h].wait()

                @pl.loop(0, hd // st)
                def _(i):
                    row = pl.ds(pl.multiple_of(i * st, st), st)
                    dwv[2 * k + h, row, :] = dwv[2 * k + h, row, :] + cst[h, row, :]

    with sc("own_in"):
        for k in range(3):
            local[k].wait()
            if k < 2:
                xo[k].start()
                yo[k].start()
        yd[0].start()
        for cp in local[3:]:
            cp.wait()
    for j in range(2):
        acopy(0, 1, j).start()

    @mid
    def _():
        for j in range(2):
            bcopy(0, 2, j).start()

    for k in range(3):
        co[k].start()

    eye[...] = (
        lax.broadcasted_iota(jnp.int32, (hd, hd), 0) == lax.broadcasted_iota(jnp.int32, (hd, hd), 1)
    ).astype(f32).astype(bf)

    with sc("xt0"):
        transpose_x(1, 0, 1)

    def pass_on(s, j):
        with sc(f"rows{s}_{j}"):
            got(s, j)
        if s == 1:
            bcopy(1, 3, j).start()
        else:
            acopy(s, s, j).start()

    with sc("gx0"):
        xo[0].wait_recv()
        cx[0].start()
        yo[0].wait_recv()
    rg.start()
    cy[0].start()

    @mid
    def _():
        pass_on(1, 0)
        pass_on(2, 0)

    with sc("gx1"):
        xo[1].wait_recv()
        for cp in rua:
            cp.start()
        yd[1].start()
        cx[1].start()
        yo[1].wait_recv()
    for cp in rub:
        cp.start()
    for h in range(2):
        xd[h].start()
    cy[1].start()

    @mid
    def _():
        pass_on(1, 1)
        pass_on(2, 1)

    @end
    def _():
        with sc("e_rows1"):
            got(1, 0)

    with sc("gc0"):
        for cp in (*co[:2], *cx):
            cp.wait_recv()
    part_ab(1, 0)
    part_ab(0, 0)
    with sc("gyd"):
        yd[0].wait_recv()
        cyd[0].start()
        rg.wait_recv()
        crg.start()
    with sc("gc1"):
        for cp in (*cy, crg):
            cp.wait_recv()
    part_ab(1, 1, 1)
    co[2].wait_recv()

    @end
    def _():
        @pl.loop(0, 2)
        def _(i):
            n = pl.ds(pl.multiple_of(2 * i * kd, kd), hd)
            zs[2 * i, :, pl.ds(0, hd)] = mm(act[2, rows(1), pl.ds(0, kf)], wd[pl.ds(0, kf), n])

    @mid
    def _():
        pass_on(3, 0)

    with sc("gru"):
        for cp, fwd in zip((*rua[:1], *rub[:1], *rua[1:], *rub[1:]), (*crua[:1], *crub[:1], *crua[1:], *crub[1:])):
            cp.wait_recv()
            fwd.start()
    with sc("gc2"):
        for cp in (*crua, *crub):
            cp.wait_recv()
    part_ab(1, 1, 2)
    with sc("gc3"):
        cyd[0].wait_recv()

    def early_half(h):
        with sc(f"early1_{h}"):
            @pl.loop(0, 2)
            def _(i):
                r = 2 * i
                col = pl.ds(h * hd, hd)
                n = pl.ds(pl.multiple_of(r * kd + h * hd, hd), hd)
                if h == 0:
                    v = zs[r, :, col] + mm(act[2, rows(1), pl.ds(kf, kf)], wd[pl.ds(kf, kf), n])
                else:
                    v = mm(act[2, rows(1), :], wd[:, n])
                zs[r, :, col] = v
                remote(zs.at[r, :, col], zl.at[0, r, :, col], zsend.at[r], zrecv.at[0, r], dev_a).start()

    def early(s, odd):
        with sc(f"early{s}_{odd}"):
            @pl.loop(0, 2)
            def _(i):
                r = 2 * i + odd
                chunk(0, s, r, s - 1, None, True)
                zcopy(s - 1, 0, r, s - 1, dev_a).start()

    @end
    def _():
        early_half(0)
        with sc("e_rows2"):
            got(2, 0)

    part_ab(2, 0)
    with sc("gd0"):
        yd[1].wait_recv()
        cyd[1].start()
        xd[0].wait_recv()
        rd[0].start()
        cxd[0].start()
        cyd[1].wait_recv()

    @end
    def _():
        early_half(1)

    part_ab(2, 1)

    @end
    def _():
        early(2, 0)

    @mid
    def _():
        pass_on(3, 1)

    with sc("gd1"):
        xd[1].wait_recv()
        rd[1].start()
        cxd[1].start()
    part_ab(0, 1)
    with sc("gd2"):
        rd[0].wait_recv()
        crd[0].start()
    transpose_x(1, 1, 3)
    keep_h(0, 3)
    with sc("gd3"):
        rd[1].wait_recv()
        crd[1].start()
        for cp in (*cxd, *crd):
            cp.wait_recv()

    @end
    def _():
        early(1, 1)
        early(2, 1)
        got(1, 1)
        got(2, 1)
        with sc("e_rows3"):
            got(3, 0)

    part_ab(3, 0)
    part_ab(3, 1)
    flush(0)
    flush(1)
    gload(1)
    transpose_x(1, 3, 4)
    keep_h(3, 4)
    front_g(1, 0)
    front_g(0, 2)
    front_g(2, 3)
    far_start(0, 3)

    @end
    def _():
        with sc("e_rows3"):
            got(3, 1)

    far_start(3, 4)
    half_g(3, 1, None)
    near_load(1, 0)
    half_g(3, 0, None)
    near_load(1, 1)

    @pl.loop(0, 2)
    def _(j):
        near_unit(1, j)
        ncopy(j).start()

    for j in range(2):
        near_done(1, j)
    dw(1, 2, 2)

    @end
    def _():
        jobs((0, 3, 0, None, 2, dev_a, False))

    @mid
    def _():
        jobs((0, 2, 0, 1, 3, dev_b, True))

    with sc("xtb"):
        transpose_x(0, 0, 4)
    dw(0, 0, 0)
    for u in range(3):
        fcopy(u).wait_send()
    for cp in wcopies:
        cp.wait_send()
    for j in range(2):
        acopy(0, 1, j).wait_send()

    @mid
    def _():
        for j in range(2):
            bcopy(0, 2, j).wait_send()
            bcopy(1, 3, j).wait_send()
            acopy(2, 2, j).wait_send()
            acopy(3, 3, j).wait_send()

    @end
    def _():
        jobs((1, 3, 1, None, 2, dev_a, False))
        second(0)
        second(1)
        second(2)
        jobs((1, 2, 0, None, 1, dev_a, False))
        third(0)
        third(1)
        jobs((1, 1, 1, None, 0, dev_a, False))
        third(2)
        finish(0, (0,))
        last_part()
        fourth(0)
        finish(1, (0,), 0, 2)
        fourth(1)
        finish(1, (0,), 2, 3)
        fourth(2)

    @mid
    def _():
        jobs((0, 3, 1, 2, 4, dev_b, True))
        second(0)
        second(1)
        second(2)
        jobs((0, 1, 0, 4, 0, dev_a, False), (1, 3, 1, 2, 4, dev_b, False))
        third(0)
        third(1)
        jobs((1, 1, 0, 4, 0, dev_a, False), (1, 2, 1, 1, 3, dev_b, False))
        third(2)
        finish(0, (0, 3))
        fourth(0)
        fourth(1)
        last_part()
        finish(1, (0, 3), 0, 3)
        fourth(2)
        zcopy(3, 1, 3, 0, dev_a).wait_recv()

    zcopy(0, 1, 3, 0, dev_a).wait_recv()

    with sc("drain"):
        for half in range(2):
            for r in range(4):
                zcopy(0, 0, r, half, dev_a).wait_send()
        for i in range(6):
            xcopy1(i, 0).wait_send()
            ycopy1(i, 0).wait_send()
        for k in range(3):
            ycopy2(k).wait_send()
            xcopy2(k).wait_send()


def fused(x, dy, wg, wu, wd):
    nr, d = x.shape
    kd, kf = wg.shape
    f, hd = 2 * kf, kd // 2
    hbm = pl.BlockSpec(memory_space=pl.ANY)
    sds = jax.ShapeDtypeStruct
    out_shape = (
        pltpu.VMEM((4 * nr, d), bf), pltpu.VMEM((4 * nr, d), bf), pltpu.VMEM((6, hd, kf), f32),
        sds((5, 8, nr, kd), f32), sds((6, hd, kf), f32), sds((6, hd, kf), f32),
        sds((24, hd, kf), f32), sds((24, hd, kf), f32),
        sds((6, hd, kf), f32), sds((6, hd, kf), f32), sds((4, 2, 2, nr, kf), f32),
    )
    dma = pltpu.SemaphoreType.DMA
    return pl.pallas_call(
        kernel,
        name="fused",
        out_shape=out_shape,
        in_specs=[hbm] * 5,
        out_specs=(pl.BlockSpec(memory_space=pltpu.VMEM),) * 3 + (hbm,) * (len(out_shape) - 3),
        scratch_shapes=[
            pltpu.VMEM((d, f), bf), pltpu.VMEM((d, f), bf), pltpu.VMEM((f, d), bf),
            pltpu.VMEM((3, 4 * nr, f), bf),
            pltpu.VMEM((8, nr, kd), f32), pltpu.VMEM((2, kd, 4 * nr), bf), pltpu.VMEM((f, 4 * nr), bf),
            pltpu.VMEM((hd, hd), bf),
            pltpu.VMEM((2, hd, kf), f32),
            dma((49,)), dma((41,)), dma((11,)), dma((8,)), dma((5, 8)), dma((2,)), dma((3,)), dma((24,)), dma((2,)),
            dma((2,)), dma((6,)), dma((6,)), dma((6,)), dma((6,)), dma((6,)), dma((6,)), dma((2,)), dma((4,)),
        ],
        compiler_params=pltpu.CompilerParams(collective_id=0, has_side_effects=True, vmem_limit_bytes=VMEM_LIMIT - 14 * 2**20),
    )(x, dy, wg, wu, wd)


def tail_kernel(xa, dya, dwv, zl, y, dx, dwg, dwu, dwd, buf, out, sem, lsem):
    dp = lax.axis_index("dp")
    z = lax.axis_index("tp") // 2
    is_mid = (z == 1) | (z == 2)
    nr, kd = y.shape[0], dwd.shape[1]
    hd = kd // 2
    srcs = (zl.at[1, 7], zl.at[0, 7], zl.at[3, 7])
    loads = [pltpu.make_async_copy(v, buf.at[i], lsem.at[i]) for i, v in enumerate(srcs)]
    loads[0].start()
    loads[1].start()

    @pl.when(is_mid)
    def _():
        loads[2].start()

    copies = []
    for k in range(3):
        for h in range(2):
            v = dwv.at[2 * k + h]
            if k > 0:
                copies.append((v, (dwg, dwu)[k - 1].at[pl.ds(h * hd, hd)]))
            else:
                for q in range(2):
                    copies.append((v.at[:, pl.ds(q * kd, kd)], dwd.at[pl.ds((2 * h + q) * hd, hd)]))
    for src, dst, n in ((xa, y, 4), (dya, dx, 3)):
        for r in range(n):
            copies.append((src.at[pl.ds(nr, nr), pl.ds(r * kd, kd)], dst.at[:, natural(dp, r, kd)]))
    copies.append((out, dx.at[:, natural(dp, 3, kd)]))
    copies = [pltpu.make_async_copy(s, t, sem.at[i]) for i, (s, t) in enumerate(copies)]
    for c in copies[:-1]:
        c.start()
    loads[0].wait()
    loads[1].wait()
    buf[0] = buf[0] + buf[1]

    @pl.when(is_mid)
    def _():
        loads[2].wait()
        buf[0] = buf[0] + buf[2]

    out[...] = buf[0].astype(bf)
    copies[-1].start()
    for c in copies:
        c.wait()


def tail(xa, dya, dwv, zl, nr, kd, kf):
    hbm = pl.BlockSpec(memory_space=pl.ANY)
    sds = jax.ShapeDtypeStruct
    d = xa.shape[1]
    dma = pltpu.SemaphoreType.DMA
    return pl.pallas_call(
        tail_kernel,
        name="tail",
        out_shape=(sds((nr, d), bf), sds((nr, d), bf), sds((kd, kf), f32), sds((kd, kf), f32), sds((kf, kd), f32)),
        in_specs=[hbm] * 4,
        out_specs=(hbm,) * 5,
        scratch_shapes=[pltpu.VMEM((3, nr, kd), f32), pltpu.VMEM((nr, kd), bf), dma((16,)), dma((3,))],
        compiler_params=pltpu.CompilerParams(vmem_limit_bytes=VMEM_LIMIT - 27 * 2**20),
    )(xa, dya, dwv, zl)


def solution(mesh):
    rows = P(("dp", "tp"), None)
    wsp = P("dp", "tp")
    dsp = P("tp", "dp")

    def local(x, w_gate, w_up, w_down, dy):
        return tail(*fused(x, dy, w_gate, w_up, w_down)[:4], x.shape[0], *w_gate.shape)

    return jax.shard_map(local, mesh=mesh, in_specs=(rows, wsp, wsp, dsp, rows), out_specs=(rows, rows, wsp, wsp, dsp), check_vma=False)
```

profile of v0, /device:TPU:0, one launch (start us, length us, event | category | flops | bytes accessed | tf_op | source)
XLA Modules:
  0.0 360.8 jit_solution(14911718766231944039)
XLA Ops:
  0.6 356.5 %fused.1 = (bf16[1024,2048]{1,0:T(8,128)(2,1)S(1)}, bf16[1024,2048]{1,0:T(8,128)(2,1)S(1)}, f32[6,256,1024]{2,1,0:T(8,128)S(1)}, f32[5,8,256,512]{3,2,1,0:T(8,12...) custom-call(bf16[256,2048]{1,0:T(8,128)(2,1)} %x_in.1, ...), custom_call_target="tpu_custom_call" | custom-call | tf_op jit(solution)/shard_map/fused/pallas_call | solution.py:819
  357.2 3.4 tail.1
where the time goes:
time: 362 us; the launch traced here: 361 us
  Pallas kernels  360 us (99%)
    pallas_call x1, Pallas kernels, fused(): pl.pallas_call(kernel, name='fused', out_shape=out_shape, in_specs=[hbm]...  357 us

commit v1 on v0

--- a/solution.py
+++ b/solution.py
@@ -787,20 +787,23 @@
         last_part()
         finish(1, (0, 3), 0, 3)
         fourth(2)
-        zcopy(3, 1, 3, 0, dev_a).wait_recv()
-
-    zcopy(0, 1, 3, 0, dev_a).wait_recv()
 
     with sc("drain"):
-        for half in range(2):
-            for r in range(4):
-                zcopy(0, 0, r, half, dev_a).wait_send()
         for i in range(6):
             xcopy1(i, 0).wait_send()
             ycopy1(i, 0).wait_send()
         for k in range(3):
             ycopy2(k).wait_send()
             xcopy2(k).wait_send()
+        for half in range(2):
+            for r in range(4):
+                zcopy(0, 0, r, half, dev_a).wait_send()
+
+        @mid
+        def _():
+            zcopy(3, 1, 3, 0, dev_a).wait_recv()
+
+        zcopy(0, 1, 3, 0, dev_a).wait_recv()
 
 
 def fused(x, dy, wg, wu, wd):

time: 362 us -> 362 us (level)
  no operation moved by 1% of the time
where the time goes in v1:
time: 362 us; the launch traced here: 361 us
  Pallas kernels  360 us (99%)
    pallas_call x1, Pallas kernels, fused(): pl.pallas_call(kernel, name='fused', out_shape=out_shape, in_specs=[hbm]...  356 us

profile of v1, /device:TPU:0, one launch (start us, length us, event | category | flops | bytes accessed | tf_op | source)
XLA Modules:
  0.0 360.7 jit_solution(2093914868584564240)
XLA Ops:
  0.6 356.5 %fused.1 = (bf16[1024,2048]{1,0:T(8,128)(2,1)S(1)}, bf16[1024,2048]{1,0:T(8,128)(2,1)S(1)}, f32[6,256,1024]{2,1,0:T(8,128)S(1)}, f32[5,8,256,512]{3,2,1,0:T(8,12...) custom-call(bf16[256,2048]{1,0:T(8,128)(2,1)} %x_in.1, ...), custom_call_target="tpu_custom_call" | custom-call | tf_op jit(solution)/shard_map/fused/pallas_call | solution.py:822
  357.1 3.4 tail.1

commit v2 on v1

--- a/solution.py
+++ b/solution.py
@@ -191,7 +191,7 @@
             fst[at] = sa
             nst[at] = b * sig * (1.0 + a * (1.0 - sig))
 
-        m = 2 if step == 2 and kf // ft > 1 else 1
+        m = min(4, kf // ft) if step == 2 else 1
 
         @pl.loop(0, kf // ft // m)
         def _(i):

time: 362 us -> 362 us (level)
  no operation moved by 1% of the time
where the time goes in v2:
time: 362 us; the launch traced here: 361 us
  Pallas kernels  360 us (99%)
    pallas_call x1, Pallas kernels, fused(): pl.pallas_call(kernel, name='fused', out_shape=out_shape, in_specs=[hbm]...  356 us

profile of v2, /device:TPU:0, one launch (start us, length us, event | category | flops | bytes accessed | tf_op | source)
XLA Modules:
  0.0 360.7 jit_solution(15019776729869926076)
XLA Ops:
  0.6 356.5 %fused.1 = (bf16[1024,2048]{1,0:T(8,128)(2,1)S(1)}, bf16[1024,2048]{1,0:T(8,128)(2,1)S(1)}, f32[6,256,1024]{2,1,0:T(8,128)S(1)}, f32[5,8,256,512]{3,2,1,0:T(8,12...) custom-call(bf16[256,2048]{1,0:T(8,128)(2,1)} %x_in.1, ...), custom_call_target="tpu_custom_call" | custom-call | tf_op jit(solution)/shard_map/fused/pallas_call | solution.py:822
  357.1 3.4 tail.1
